TPU v7x, 32 devices: a whole 2x2x4 slice. The times are simulated.
32 devices in a mesh: dp: 2 (over x), tp: 4 (over z), cp: 4 (over y, core).
Axes of the slice: x: 2, y: 2, z: 4, core: 2. Of those that a mesh axis runs over, the one named last changes fastest.
Arguments:
- tokens: bfloat16 [6144, 3584], P(('dp', 'tp', 'cp')), parts along dimension 0
- norm_attn: bfloat16 [2, 3584], replicated
- norm_mlp: bfloat16 [2, 3584], replicated
- w_q: bfloat16 [2, 3584, 28, 128], P(None, None, 'tp')
- w_k: bfloat16 [2, 3584, 512], P(None, None, 'tp')
- w_v: bfloat16 [2, 3584, 512], P(None, None, 'tp')
- w_o: bfloat16 [2, 28, 128, 3584], P(None, 'tp')
- w_gate: bfloat16 [2, 3584, 18944], P(None, None, 'tp')
- w_up: bfloat16 [2, 3584, 18944], P(None, None, 'tp')
- w_down: bfloat16 [2, 18944, 3584], P(None, 'tp')
Outputs:
- output: bfloat16 [6144, 3584], P(('dp', 'tp', 'cp')), parts along dimension 0
There are 2 independent parts. A program takes and returns all parts, laid end to end along the dimension named above; an argument that names none is the same for every part.
All inputs are finite; a program needn't handle non-finite values.
Results may differ from a plain program's by a relative error of at most 0.02.
Values are sent between devices in bfloat16 or wider.
A program may use at most 1 GiB of HBM per device.

v0:
```python
import math
import jax
import jax.numpy as jnp
from jax import lax
from jax.sharding import PartitionSpec as P, NamedSharding


def rms_norm(hidden, gain):
    hidden_f = hidden.astype(jnp.float32)
    inv_rms = lax.rsqrt(jnp.mean(hidden_f * hidden_f, axis=-1, keepdims=True) + 1e-5)
    return (hidden_f * inv_rms * gain.astype(jnp.float32)).astype(jnp.bfloat16)


def rotary(values, positions):
    half_dim = values.shape[-1] // 2
    inv_freq = 500000.0 ** (-(jnp.arange(half_dim, dtype=jnp.float32) * 2.0 / values.shape[-1]))
    angles = positions.astype(jnp.float32)[:, None] * inv_freq[None, :]
    cos_ang = jnp.cos(angles)[:, None, :]
    sin_ang = jnp.sin(angles)[:, None, :]
    first = values[..., :half_dim]
    second = values[..., half_dim:]
    return jnp.concatenate([first * cos_ang - second * sin_ang, second * cos_ang + first * sin_ang], axis=-1)


def seg_positions(dev_ids, rows, dev_total):
    offset = jnp.arange(rows)
    half_len = rows // 2
    seg_idx = jnp.where(offset < half_len, dev_ids[..., None], 2 * dev_total - 1 - dev_ids[..., None])
    return seg_idx * half_len + offset % half_len


def attend(queries, keys_all, values_all, q_pos, k_pos, block_rows):
    rows, kv_loc, group, head_dim = queries.shape
    scale = 1.0 / math.sqrt(head_dim)
    q_blocks = queries.reshape(rows // block_rows, block_rows, kv_loc, group, head_dim)
    pos_blocks = q_pos.reshape(rows // block_rows, block_rows)

    def one_block(block):
        q_blk, pos_blk = block
        scores = jnp.einsum('bkgd,tkd->bkgt', q_blk, keys_all, preferred_element_type=jnp.float32) * scale
        visible = k_pos[None, None, None, :] <= pos_blk[:, None, None, None]
        scores = jnp.where(visible, scores, -jnp.inf)
        weights = jnp.exp(scores - jnp.max(scores, axis=-1, keepdims=True))
        row_sum = jnp.sum(weights, axis=-1, keepdims=True)
        mixed = jnp.einsum('bkgt,tkd->bkgd', weights.astype(jnp.bfloat16), values_all, preferred_element_type=jnp.float32)
        return (mixed / row_sum).astype(jnp.bfloat16)

    return lax.map(one_block, (q_blocks, pos_blocks)).reshape(rows, kv_loc * group, head_dim)


def solution(mesh):
    tp_size = mesh.shape['tp']
    cp_size = mesh.shape['cp']
    dev_total = tp_size * cp_size
    row_spec = P(('dp', 'tp', 'cp'), None)
    gain_spec = P(None, None)
    q_spec = P(None, None, 'tp', None)
    col_spec = P(None, None, 'tp')
    o_spec = P(None, 'tp', None, None)
    down_spec = P(None, 'tp', None)

    def body(tokens, norm_attn, norm_mlp, w_q, w_k, w_v, w_o, w_gate, w_up, w_down):
        rows = tokens.shape[0]
        heads_loc = w_q.shape[2]
        head_dim = w_q.shape[3]
        kv_cols = w_k.shape[2]
        tp_idx = lax.axis_index('tp')
        cp_idx = lax.axis_index('cp')
        tp_devs = jnp.arange(tp_size) * cp_size + cp_idx
        pos_rows = seg_positions(tp_devs, rows, dev_total).reshape(tp_size * rows)
        key_devs = jnp.arange(cp_size)[:, None] + jnp.arange(tp_size)[None, :] * cp_size
        pos_keys = seg_positions(key_devs, rows, dev_total).reshape(dev_total * rows)
        hidden = tokens
        for layer_idx in range(w_q.shape[0]):
            normed = lax.all_gather(rms_norm(hidden, norm_attn[layer_idx]), 'tp', axis=0, tiled=True)
            q_proj = jnp.einsum('rd,dhe->rhe', normed, w_q[layer_idx], preferred_element_type=jnp.float32)
            queries = rotary(q_proj, pos_rows).astype(jnp.bfloat16)
            wk_loc = w_k[layer_idx]
            wv_loc = w_v[layer_idx]
            if kv_cols >= head_dim:
                kv_loc = kv_cols // head_dim
            else:
                kv_total = kv_cols * tp_size // head_dim
                start = (tp_idx * kv_total // tp_size) * head_dim
                wk_loc = lax.dynamic_slice_in_dim(lax.all_gather(wk_loc, 'tp', axis=1, tiled=True), start, head_dim, axis=1)
                wv_loc = lax.dynamic_slice_in_dim(lax.all_gather(wv_loc, 'tp', axis=1, tiled=True), start, head_dim, axis=1)
                kv_loc = 1
            k_proj = jnp.dot(normed, wk_loc, preferred_element_type=jnp.float32)
            keys_loc = rotary(k_proj.reshape(tp_size * rows, kv_loc, head_dim), pos_rows).astype(jnp.bfloat16)
            values_loc = jnp.dot(normed, wv_loc, preferred_element_type=jnp.float32).astype(jnp.bfloat16).reshape(tp_size * rows, kv_loc, head_dim)
            keys_all = lax.all_gather(keys_loc, 'cp', axis=0, tiled=True)
            values_all = lax.all_gather(values_loc, 'cp', axis=0, tiled=True)
            grouped = queries.reshape(tp_size * rows, kv_loc, heads_loc // kv_loc, head_dim)
            mixed = attend(grouped, keys_all, values_all, pos_rows, pos_keys, rows // 2)
            attn_part = jnp.einsum('rhe,hed->rd', mixed, w_o[layer_idx], preferred_element_type=jnp.float32)
            attn_out = lax.psum_scatter(attn_part, 'tp', scatter_dimension=0, tiled=True)
            hidden_mid = (hidden.astype(jnp.float32) + attn_out).astype(jnp.bfloat16)
            normed_mlp = lax.all_gather(rms_norm(hidden_mid, norm_mlp[layer_idx]), 'tp', axis=0, tiled=True)
            gate_pre = jnp.dot(normed_mlp, w_gate[layer_idx], preferred_element_type=jnp.float32)
            up_proj = jnp.dot(normed_mlp, w_up[layer_idx], preferred_element_type=jnp.float32)
            hidden_act = (jax.nn.silu(gate_pre) * up_proj).astype(jnp.bfloat16)
            mlp_part = jnp.dot(hidden_act, w_down[layer_idx], preferred_element_type=jnp.float32)
            mlp_out = lax.psum_scatter(mlp_part, 'tp', scatter_dimension=0, tiled=True)
            hidden = (hidden_mid.astype(jnp.float32) + mlp_out).astype(jnp.bfloat16)
        return hidden

    return jax.shard_map(
        body,
        mesh=mesh,
        in_specs=(row_spec, gain_spec, gain_spec, q_spec, col_spec, col_spec, o_spec, col_spec, col_spec, down_spec),
        out_specs=row_spec,
        check_vma=False,
    )
```

profile of v0, /device:TPU:0, one launch (start us, length us, event | category | flops | bytes accessed | tf_op | source)
XLA Modules:
  0.0 1661.3 jit_solution(13035688992120665078)
XLA Ops:
  9.7 2.8 fusion.100
  13.3 10.2 fusion.144
  23.6 9.5 copy.33
  35.0 82.4 %all-gather.7.cloned.1.call-done = bf16[768,3584]{1,0:T(8,128)(2,1)} async-done(((bf16[192,3584]{1,0:T(8,128)(2,1)}), bf16[768,3584]{1,0:T(8,128)(2,1)}) %all-gather.7.cloned.1.call-update) | async-done | bytes 5505040 | tf_op jit(solution)/shard_map/all_gather | solution.py:75
  117.3 8.9 fusion.145
  133.0 4.7 convolution_bitcast_fusion.3
  138.6 8.6 all_gather.25
  148.7 4.4 convolution_convert_fusion.1
  153.1 8.9 all-gather
  164.0 64.3 %while.22 = (s32[]{:T(128)}, bf16[8,96,1,7,128]{4,1,0,3,2:T(8,128)(2,1)S(1)}, s32[8,96]{1,0:T(8,128)}, bf16[8,96,1,7,128]{4,1,3,2,0:T(8,128)(2,1)}, bf16[3072,1,...) while((s32[]{:T(128)}, ...), condition=%wide.region_4.5_spmd.clone, body=%wide.region_1.4_spmd.clone.sunk | while | flops 1080147712 | bytes 31083216 | solution.py:48
  165.1 2.5 fusion.200
  173.1 2.5 fusion.200
  181.2 2.5 fusion.200
  189.2 2.5 fusion.200
  197.2 2.5 fusion.200
  205.3 2.5 fusion.200
  213.3 2.5 fusion.200
  221.3 2.5 fusion.200
  228.3 10.4 convolution_bitcast_fusion.1
  240.1 183.2 %reduce-scatter.5.cloned.1.call-done = f32[192,3584]{1,0:T(8,128)} async-done(((f32[768,3584]{1,0:T(8,128)}), f32[192,3584]{1,0:T(8,128)}) %reduce-scatter.5.cloned.1.call-update) | async-done | bytes 2752528 | tf_op jit(solution)/shard_map/reduce_scatter | solution.py:96
  427.6 102.4 %all-gather.9.cloned.1.call-done = bf16[768,3584]{1,0:T(8,128)(2,1)} async-done(((bf16[192,3584]{1,0:T(8,128)(2,1)}), bf16[768,3584]{1,0:T(8,128)(2,1)}) %all-gather.9.cloned.1.call-update) | async-done | bytes 5505040 | tf_op jit(solution)/shard_map/all_gather | solution.py:98
  530.0 35.3 %fusion.76 = f32[768,4736]{1,0:T(8,128)} fusion(bf16[768,3584]{1,0:T(8,128)(2,1)} %all-gather.9.cloned.1.call-done, bf16[2,3584,4736]{2,1,0:T(8,128)(2,1)} %param.21), kind=kOutput, calls=%fused_computation.62 | convolution fusion | flops 26071793664 | bytes 54001664 | tf_op jit(solution)/shard_map/dot_general | solution.py:99
  565.2 37.4 %multiply_convert_fusion.1.clone.5 = bf16[768,4736]{1,0:T(8,128)(2,1)} fusion(f32[768,4736]{1,0:T(8,128)} %fusion.76, bf16[768,3584]{1,0:T(8,128)(2,1)} %all-gather.9.cloned.1.call-done, bf16[2,3584,4736]{2,1,0:T(8,128)(2,1)} %param.22), kind=kOutput, calls=%fused_computation.71.clone.clone.clone.2 | convolution fusion | flops 26093617152 | bytes 61276160 | tf_op jit(solution)/shard_map/dot_general | solution.py:100
  602.7 33.9 %fusion.72 = f32[768,3584]{1,0:T(8,128)} fusion(bf16[2,4736,3584]{2,1,0:T(8,128)(2,1)} %param.23, bf16[768,4736]{1,0:T(8,128)(2,1)} %multiply_convert_fusion.1.clone.5), kind=kOutput, calls=%fused_computation.58 | convolution fusion | flops 26071793664 | bytes 52232192 | tf_op jit(solution)/shard_map/dot_general | solution.py:102
  636.6 184.9 %reduce-scatter.7.cloned.1.call-done = f32[192,3584]{1,0:T(8,128)} async-done(((f32[768,3584]{1,0:T(8,128)}), f32[192,3584]{1,0:T(8,128)}) %reduce-scatter.7.cloned.1.call-update) | async-done | bytes 2752528 | tf_op jit(solution)/shard_map/reduce_scatter | solution.py:103
  825.6 9.5 copy.34
  835.1 93.0 %all-gather.11.cloned.1.call-done = bf16[768,3584]{1,0:T(8,128)(2,1)} async-done(((bf16[192,3584]{1,0:T(8,128)(2,1)}), bf16[768,3584]{1,0:T(8,128)(2,1)}) %all-gather.11.cloned.1.call-update) | async-done | bytes 5505040 | tf_op jit(solution)/shard_map/all_gather | solution.py:75
  928.2 4.7 convolution_bitcast_fusion.2
  933.7 8.6 all_gather.29
  942.7 9.0 fusion.146
  957.0 2.8 concatenate.59
  959.8 2.6 copy.26
  962.4 4.5 convolution_convert_fusion
  966.9 8.9 all-gather.1
  977.9 79.9 %while.23 = (s32[]{:T(128)}, bf16[8,96,1,7,128]{4,1,0,3,2:T(8,128)(2,1)S(1)}, s32[8,96]{1,0:T(8,128)}, bf16[8,96,1,7,128]{4,1,3,2,0:T(8,128)(2,1)}, bf16[3072,1,...) while((s32[]{:T(128)}, ...), condition=%wide.region_12.13_spmd.clone, body=%wide.region_9.12_spmd.clone.sunk | while | flops 1080147712 | bytes 31083216 | solution.py:48
  981.0 2.5 fusion.206
  991.0 2.5 fusion.206
  1011.0 2.5 fusion.206
  1020.9 2.5 fusion.206
  1040.9 2.5 fusion.206
  1057.8 10.4 convolution_bitcast_fusion
  1068.3 184.5 %reduce-scatter.9.cloned.1.call-done = f32[192,3584]{1,0:T(8,128)} async-done(((f32[768,3584]{1,0:T(8,128)}), f32[192,3584]{1,0:T(8,128)}) %reduce-scatter.9.cloned.1.call-update) | async-done | bytes 2752528 | tf_op jit(solution)/shard_map/reduce_scatter | solution.py:96
  1256.9 102.5 %all-gather.13.cloned.1.call-done = bf16[768,3584]{1,0:T(8,128)(2,1)} async-done(((bf16[192,3584]{1,0:T(8,128)(2,1)}), bf16[768,3584]{1,0:T(8,128)(2,1)}) %all-gather.13.cloned.1.call-update) | async-done | bytes 5505040 | tf_op jit(solution)/shard_map/all_gather | solution.py:98
  1359.4 35.2 %fusion.70 = f32[768,4736]{1,0:T(8,128)} fusion(bf16[768,3584]{1,0:T(8,128)(2,1)} %all-gather.13.cloned.1.call-done, bf16[2,3584,4736]{2,1,0:T(8,128)(2,1)} %param.21), kind=kOutput, calls=%fused_computation.56 | convolution fusion | flops 26071793664 | bytes 54001664 | tf_op jit(solution)/shard_map/dot_general | solution.py:99
  1394.6 37.4 %multiply_convert_fusion.clone.5 = bf16[768,4736]{1,0:T(8,128)(2,1)} fusion(f32[768,4736]{1,0:T(8,128)} %fusion.70, bf16[768,3584]{1,0:T(8,128)(2,1)} %all-gather.13.cloned.1.call-done, bf16[2,3584,4736]{2,1,0:T(8,128)(2,1)} %param.22), kind=kOutput, calls=%fused_computation.70.clone.clone.clone.2 | convolution fusion | flops 26093617152 | bytes 61276160 | tf_op jit(solution)/shard_map/dot_general | solution.py:100
  1432.0 33.9 %fusion.66 = f32[768,3584]{1,0:T(8,128)} fusion(bf16[2,4736,3584]{2,1,0:T(8,128)(2,1)} %param.23, bf16[768,4736]{1,0:T(8,128)(2,1)} %multiply_convert_fusion.clone.5), kind=kOutput, calls=%fused_computation.52 | convolution fusion | flops 26071793664 | bytes 52232192 | tf_op jit(solution)/shard_map/dot_general | solution.py:102
  1465.9 185.0 %reduce-scatter.11.cloned.1.call-done = f32[192,3584]{1,0:T(8,128)} async-done(((f32[768,3584]{1,0:T(8,128)}), f32[192,3584]{1,0:T(8,128)}) %reduce-scatter.11.cloned.1.call-update) | async-done | bytes 2752528 | tf_op jit(solution)/shard_map/reduce_scatter | solution.py:103
  1650.9 3.1 fusion.113
  (235 shorter events, 150.1 us)
Async XLA Ops:
  6.5 110.8 %all-gather.7.cloned.1.call-start = ((), (), s32[]{:S(2)}) async-start(), calls=%async_computation.4 | async-start | bytes 6881280 | tf_op jit(solution)/shard_map/all_gather | solution.py:75
  12.5 410.8 %reduce-scatter.5.cloned.1.call-start = ((), (), s32[]{:S(2)}) async-start(), calls=%async_computation.5 | async-start | bytes 13762560 | tf_op jit(solution)/shard_map/reduce_scatter | solution.py:96
  12.6 0.6 copy-start.15
  13.3 124.4 %copy-start.11 = (f32[768]{0:T(1024)}, f32[768]{0:T(1024)S(1)}, u32[]{:S(2)}) copy-start(f32[768]{0:T(1024)S(1)} %convert_element_type.128) | copy-start | bytes 9220
  33.5 92.8 %copy-start.18 = (f32[64]{0:T(128)}, f32[64]{0:T(128)S(1)}, u32[]{:S(2)}) copy-start(f32[64]{0:T(128)S(1)} %negate_power_fusion) | copy-start | bytes 772
  34.9 91.3 %copy-start.2 = (f32[768,64]{0,1:T(8,128)}, f32[768,64]{0,1:T(8,128)S(1)}, u32[]{:S(2)}) copy-start(f32[768,64]{0,1:T(8,128)S(1)} %get-tuple-element.237) | copy-start | bytes 589828
  35.0 91.3 %copy-start.4 = (f32[768,64]{0,1:T(8,128)}, f32[768,64]{0,1:T(8,128)S(1)}, u32[]{:S(2)}) copy-start(f32[768,64]{0,1:T(8,128)S(1)} %get-tuple-element.238) | copy-start | bytes 589828
  133.0 4.8 copy-start.19
  148.7 15.3 copy-start.16
  167.6 2.2 copy-start.7
  175.6 2.2 copy-start.7
  183.7 2.2 copy-start.7
  191.7 2.2 copy-start.7
  199.7 2.2 copy-start.7
  207.8 2.2 copy-start.7
  215.8 2.2 copy-start.7
  223.8 2.2 copy-start.7
  228.3 10.4 copy-start.8
  228.3 10.4 copy-start.9
  228.3 10.4 copy-start.10
  238.7 0.7 copy-start.17
  238.7 184.6 %copy-start = (bf16[192,3584]{1,0:T(8,128)(2,1)S(1)}, bf16[192,3584]{1,0:T(8,128)(2,1)}, u32[]{:S(2)}) copy-start(bf16[192,3584]{1,0:T(8,128)(2,1)} %param.14) | copy-start | bytes 4128772
  238.8 291.2 %all-gather.9.cloned.1.call-start = ((), (), s32[]{:S(2)}) async-start(), calls=%async_computation.6 | async-start | bytes 6881280 | tf_op jit(solution)/shard_map/all_gather | solution.py:98
  427.1 394.4 %reduce-scatter.7.cloned.1.call-start = ((), (), s32[]{:S(2)}) async-start(), calls=%async_computation.7 | async-start | bytes 13762560 | tf_op jit(solution)/shard_map/reduce_scatter | solution.py:103
  636.5 187.3 %copy-start.13 = (f32[3584]{0:T(1024)S(1)}, f32[3584]{0:T(1024)}, u32[]{:S(2)}) copy-start(f32[3584]{0:T(1024)} %get-tuple-element.175) | copy-start | bytes 43012
  636.6 291.6 %all-gather.11.cloned.1.call-start = ((), (), s32[]{:S(2)}) async-start(), calls=%async_computation.8 | async-start | bytes 6881280 | tf_op jit(solution)/shard_map/all_gather | solution.py:75
  825.4 427.5 %reduce-scatter.9.cloned.1.call-start = ((), (), s32[]{:S(2)}) async-start(), calls=%async_computation.9 | async-start | bytes 13762560 | tf_op jit(solution)/shard_map/reduce_scatter | solution.py:96
  835.1 97.8 %copy-start.12 = (f32[768]{0:T(1024)S(1)}, f32[768]{0:T(1024)}, u32[]{:S(2)}) copy-start(f32[768]{0:T(1024)} %copy-done.11) | copy-start | bytes 9220
  835.1 97.8 %copy-start.20 = (f32[64]{0:T(128)S(1)}, f32[64]{0:T(128)}, u32[]{:S(2)}) copy-start(f32[64]{0:T(128)} %copy-done.18) | copy-start | bytes 772
  942.7 9.0 copy-start.3
  942.7 9.0 copy-start.5
  962.4 13.4 copy-start.1
  983.5 2.2 copy-start.6
  993.5 2.2 copy-start.6
  1003.5 2.2 copy-start.6
  1013.5 2.2 copy-start.6
  1023.4 2.2 copy-start.6
  1033.4 2.2 copy-start.6
  1043.4 2.2 copy-start.6
  1053.4 2.2 copy-start.6
  1068.2 186.9 %copy-start.14 = (f32[3584]{0:T(1024)S(1)}, f32[3584]{0:T(1024)}, u32[]{:S(2)}) copy-start(f32[3584]{0:T(1024)} %get-tuple-element.173) | copy-start | bytes 43012
  1068.2 291.2 %all-gather.13.cloned.1.call-start = ((), (), s32[]{:S(2)}) async-start(), calls=%async_computation.10 | async-start | bytes 6881280 | tf_op jit(solution)/shard_map/all_gather | solution.py:98
  1256.6 394.3 %reduce-scatter.11.cloned.1.call-start = ((), (), s32[]{:S(2)}) async-start(), calls=%async_computation.11 | async-start | bytes 13762560 | tf_op jit(solution)/shard_map/reduce_scatter | solution.py:103
Sparse Core Ops, SparseCore 0:
  12.7 104.6 all-gather.6
  238.9 184.3 reduce-scatter.4
  427.3 102.6 all-gather.8
  636.7 184.8 reduce-scatter.6
  825.5 102.6 all-gather.10
  1068.3 184.4 reduce-scatter.8
  1256.7 102.6 all-gather.12
  1466.0 184.8 reduce-scatter.10
where the time goes:
time: 1670 us; the launch traced here: 1660 us
  waiting for transfers between devices  1120 us (67%)
  matrix products  346 us (21%)
  other arithmetic  79.8 us (5%)
  local copies, waits for them, and re-layouts  66.3 us (4%)
  blocking collectives  35 us (2%)
    reduce_scatter x2, waiting for transfers between devices, body(): mlp_out = lax.psum_scatter(mlp_part, 'tp', scatter_dimension=0, tiled=True)  370 us
    reduce_scatter x2, waiting for transfers between devices, body(): lax.psum_scatter(attn_part, 'tp', scatter_dimension=0, tiled=True)  368 us
    all_gather x2, waiting for transfers between devices, body(): lax.all_gather(rms_norm(hidden_mid, norm_mlp[layer_idx]), 'tp', axis=0, t...  205 us
    all_gather x2, waiting for transfers between devices, body(): lax.all_gather(rms_norm(hidden, norm_attn[layer_idx]), 'tp', axis=0, tile...  175 us
    dot_general x2, matrix products, body(): jnp.dot(normed_mlp, w_up[layer_idx], preferred_element_type=jnp.float32)  74.8 us
    dot_general x2, matrix products, body(): jnp.dot(normed_mlp, w_gate[layer_idx], preferred_element_type=jnp.float32)  70.5 us
    dot_general x2, matrix products, body(): jnp.dot(hidden_act, w_down[layer_idx], preferred_element_type=jnp.float32)  67.7 us
    dot_general x16, matrix products, one_block(): jnp.einsum('bkgd,tkd->bkgt', q_blk, keys_all, preferred_element_type=jnp....  39.9 us
  transfers between devices with their start and end apart: 8, of which 8 were waited for; matrix products, arithmetic and copies ran while one was open for 2% of the time, Pallas kernels for 0%

commit v1 on v0

v1 whole, which is shorter than its diff:
```python
import functools
import math
import jax
import jax.numpy as jnp
from jax import lax
from jax.experimental import pallas as pl
from jax.experimental.pallas import tpu as pltpu
from jax.sharding import PartitionSpec as P

F32 = jnp.float32
BF16 = jnp.bfloat16
MESH = pl.DeviceIdType.MESH
UP, DOWN = 0, 1
X, O, H = 0, 1, 2
LOW, HIGH = 0, 1
SLOTS = 3
PARTS = 2
TILE = 256


def ring(i, n):
    return lax.rem(i + n, n)


def both(*conditions):
    out = conditions[0]
    for c in conditions[1:]:
        out = jnp.logical_and(out, c)
    return out


def kernel(n, m, layers, tokens, gain_a, gain_m, cos_ref, sin_ref, w_q, w_k, w_v, w_o, w_gate, w_up, w_down,
           y_out, g_x, g_o, g_h, wo_cols,
           stage, lhs, act, part, sums, scores, ks, vs, kvs, qs, x_cols, pieces, home, wbuf, row_max, row_sum, acc_ref,
           wsem, lsem, gsend, grecv, ksend, krecv, rsend, rrecv, osend, orecv, psend, precv):
    z = lax.axis_index("tp")
    c = lax.axis_index("cp")
    rows = tokens.shape[0] // 2
    d = tokens.shape[1]
    all_rows = n * rows
    hc = w_q.shape[2]
    hd = w_k.shape[2]
    heads = hc // hd
    width = d // n
    ff = w_gate.shape[2]
    above = jnp.minimum(z + 1, n - 1)
    below = jnp.maximum(z - 1, 0)

    def remote(src, dst, send, recv, **where):
        return pltpu.make_async_remote_copy(src_ref=src, dst_ref=dst, send_sem=send, recv_sem=recv, device_id=where,
                                            device_id_type=MESH)

    def row_block(p):
        return pl.ds(pl.multiple_of(p * rows, 16), rows)

    def col_block(p, w):
        return pl.ds(pl.multiple_of(p * w, 128), w)

    class Gather:
        def __init__(self, layer, half, kind, buf, own):
            self.i = (layer * 2 + half) * 3 + kind
            self.buf, self.own = buf, own

        def copy(self, way, k, plane):
            src = self.own if k == 0 else self.buf.at[plane]
            return remote(src, self.buf.at[plane], gsend.at[self.i, way, k], grecv.at[self.i, way, k],
                          tp=above if way == UP else below)

        def start(self):
            @pl.when(z < n - 1)
            def _():
                self.copy(UP, 0, z).start()

            @pl.when(z > 0)
            def _():
                self.copy(DOWN, 0, z).start()

        def event(self, k):
            up, down = jnp.maximum(z - k, 0), jnp.minimum(z + k, n - 1)

            @pl.when(z >= k)
            def _():
                self.copy(UP, k - 1, up).wait_recv()

            if k < n - 1:
                @pl.when(both(z >= k, z < n - 1))
                def _():
                    self.copy(UP, k, up).start()

            @pl.when(z + k < n)
            def _():
                self.copy(DOWN, k - 1, down).wait_recv()

            if k < n - 1:
                @pl.when(both(z + k < n, z > 0))
                def _():
                    self.copy(DOWN, k, down).start()

        def drain(self, ks):
            for k in ks:
                @pl.when(both(z >= k, z < n - 1))
                def _(k=k):
                    self.copy(UP, k, z).wait_send()

                @pl.when(both(z + k < n, z > 0))
                def _(k=k):
                    self.copy(DOWN, k, z).wait_send()

    def own_x(layer, half):
        return tokens.at[pl.ds(half * rows, rows)] if layer == 0 else home.at[half]

    gx = {(l, h): Gather(l, h, X, g_x.at[l, h], own_x(l, h)) for l in range(layers) for h in (LOW, HIGH)}
    go = {(l, h): Gather(l, h, O, g_o.at[l, h], pieces.at[h]) for l in range(layers) for h in (LOW, HIGH)}
    gh = {(l, h): Gather(l, h, H, g_h.at[l, h], pieces.at[h]) for l in range(layers) for h in (LOW, HIGH)}

    def load(buf, own, where):
        copies = [pltpu.make_async_copy(own, stage.at[where(z)], lsem.at[0])]
        for k in range(1, n):
            p = ring(z + k, n)
            copies.append(pltpu.make_async_copy(buf.at[p], stage.at[where(p)], lsem.at[k]))
        for copy in copies:
            copy.start()
        for copy in copies:
            copy.wait()

    def load_rows(gather):
        load(gather.buf, gather.own, row_block)

    def load_cols(gather, w):
        load(gather.buf, gather.own, lambda p: (slice(None), col_block(p, w)))

    def norm(gain):
        step = 32

        @pl.loop(0, all_rows // step)
        def _(i):
            r = pl.ds(pl.multiple_of(i * step, step), step)
            x = stage[r].astype(F32)
            inv = lax.rsqrt(jnp.mean(x * x, axis=-1, keepdims=True) + 1e-5)
            lhs[r] = (x * inv * gain[...].astype(F32)).astype(BF16)

    def norm_x(layer, half):
        load_rows(gx[layer, half])
        norm(gain_a.at[pl.ds(layer, 1)])
        x_cols[half] = stage[:, col_block(z, width)]

    def norm_h(layer, half):
        load_cols(gh[layer, half], width)
        norm(gain_m.at[pl.ds(layer, 1)])
        gh[layer, half].drain((0,))
        if layer > 0:
            gx[layer, half].drain((0,))
        home[half] = stage[row_block(z)]

    class Op:
        base = None

        def start(self, i, slot):
            for copy in self.copies(i, slot):
                copy.start()

        def prefetch(self):
            for i in range(2):
                self.start(i, (self.base + i) % SLOTS)

        def run(self, follow, hooks):
            @pl.loop(0, self.tiles)
            def _(i):
                for at, event in hooks:
                    pl.when(i == at)(event)
                slot, later = lax.rem(self.base + i, SLOTS), lax.rem(self.base + i + 2, SLOTS)

                @pl.when(i + 2 < self.tiles)
                def _():
                    self.start(i + 2, later)

                if follow is not None:
                    @pl.when(i + 2 >= self.tiles)
                    def _():
                        follow.start(i + 2 - self.tiles, later)

                for copy in self.copies(i, slot):
                    copy.wait()
                self.compute(i, slot)

    def dot(a, slot, depth):
        return jnp.dot(a, wbuf[slot, :depth], preferred_element_type=F32)

    def tile_start(i, total):
        return pl.multiple_of(jnp.minimum(i * TILE, total - TILE), 128)

    class Qkv(Op):
        def __init__(self, layer, half):
            self.layer, self.half = layer, half
            self.tiles = 1 + -(-hc // TILE)

        def start(self, i, slot):
            def pair(a, b):
                pltpu.make_async_copy(a, wbuf.at[slot, pl.ds(0, d), pl.ds(0, hd)], wsem.at[slot, 0]).start()
                pltpu.make_async_copy(b, wbuf.at[slot, pl.ds(0, d), pl.ds(hd, hd)], wsem.at[slot, 1]).start()

            @pl.when(i == 0)
            def _():
                pair(w_k.at[self.layer], w_v.at[self.layer])

            @pl.when(i > 0)
            def _():
                at = tile_start(i - 1, hc)
                pair(w_q.at[self.layer, :, pl.ds(at, hd)], w_q.at[self.layer, :, pl.ds(at + hd, hd)])

        def copies(self, i, slot):
            return [pltpu.make_async_copy(w_k.at[self.layer], wbuf.at[slot, pl.ds(0, d), pl.ds(j * hd, hd)], wsem.at[slot, j])
                    for j in range(2)]

        def compute(self, i, slot):
            out = dot(lhs[...], slot, d)

            def turned(x):
                return (x * cos_ref[self.half] + pltpu.roll(x, hd // 2, 1) * sin_ref[self.half]).astype(BF16)

            @pl.when(i == 0)
            def _():
                kvs[self.layer, self.half, 0, :, :hd] = turned(out[:, :hd])
                kvs[self.layer, self.half, 0, :, hd:] = out[:, hd:].astype(BF16)

            @pl.when(i > 0)
            def _():
                h = tile_start(i - 1, hc) // hd
                for j in range(2):
                    q = turned(out[:, j * hd : (j + 1) * hd])
                    for p in range(n):
                        qs[p, row_block(h + j)] = q[p * rows : (p + 1) * rows]

    class Wo(Op):
        def __init__(self, layer, half):
            self.layer, self.half = layer, half
            self.tiles = -(-width // TILE)

        def copies(self, i, slot):
            at = tile_start(i, width)
            out = [pltpu.make_async_copy(w_o.at[self.layer, :, pl.ds(pl.multiple_of(z * width + at, 128), TILE)],
                                         wbuf.at[slot, pl.ds(pl.multiple_of(z * hc, 128), hc)], wsem.at[slot, 0])]
            for k in range(1, n):
                p = ring(z + k, n)
                block = pl.ds(pl.multiple_of(p * hc, 128), hc)
                out.append(pltpu.make_async_copy(wo_cols.at[self.layer, block, pl.ds(at, TILE)], wbuf.at[slot, block],
                                                 wsem.at[slot, k]))
            return out

        def compute(self, i, slot):
            cols = pl.ds(tile_start(i, width), TILE)
            out = dot(stage[...], slot, d) + x_cols[self.half, :, cols].astype(F32)
            pieces[self.half, :, cols] = out.astype(BF16)

    class GateUp(Op):
        def __init__(self, layer, half):
            self.layer, self.half = layer, half
            self.tiles = ff // 128

        def copies(self, i, slot):
            cols = pl.ds(pl.multiple_of(i * 128, 128), 128)
            return [pltpu.make_async_copy(w.at[self.layer, :, cols], wbuf.at[slot, pl.ds(0, d), pl.ds(128 * j, 128)], wsem.at[slot, j])
                    for j, w in enumerate((w_gate, w_up))]

        def compute(self, i, slot):
            out = dot(lhs[...], slot, d)
            gate = out[:, :128]
            act[:, pl.ds(pl.multiple_of(i * 128, 128), 128)] = (gate * lax.logistic(gate) * out[:, 128:]).astype(BF16)

    class Down(Op):
        def __init__(self, layer, half):
            self.layer, self.half = layer, half
            self.tiles = d // TILE

        def copies(self, i, slot):
            cols = pl.ds(pl.multiple_of(i * TILE, TILE), TILE)
            return [pltpu.make_async_copy(w_down.at[self.layer, :, cols], wbuf.at[slot, pl.ds(0, ff)], wsem.at[slot, 0])]

        def compute(self, i, slot):
            part[self.half, :, pl.ds(pl.multiple_of(i * TILE, TILE), TILE)] = dot(act[...], slot, ff)

    def kv_copy(layer, half, s):
        return remote(kvs.at[layer, half, 0], kvs.at[layer, half, s], ksend.at[layer, half, s - 1], krecv.at[layer, half, s - 1],
                      cp=ring(c + s, m))

    def kv_start(layer, half):
        for s in range(1, m):
            kv_copy(layer, half, s).start()

    def kv_wait(layer, half):
        for s in range(1, m):
            kv_copy(layer, half, s).wait_recv()

    def attend(layer, half):
        kv_wait(layer, half)
        keys = m * rows
        for s in range(m):
            for g in range(n):
                block = slice(g * rows, (g + 1) * rows)
                ks[half * n + g, s * rows : (s + 1) * rows] = kvs[layer, half, s, block, :hd]
                vs[half * n + g, s * rows : (s + 1) * rows] = kvs[layer, half, s, block, hd:]
        to_log2 = math.log2(math.e) / math.sqrt(hd)
        lanes = range(0, keys, 128)

        @pl.loop(0, n)
        def _(plane):
            count = plane if half == LOW else 2 * n - 1 - plane

            def group(i):
                if half == LOW:
                    return jnp.where(i == 0, plane, i - 1)
                return jnp.where(i == 0, n + plane, jnp.where(i <= n, i - 1, i + plane))

            def score(i):
                return lax.dot_general(qs[plane], ks[group(i)], (((1,), (1,)), ((), ())), preferred_element_type=F32)

            row = lax.broadcasted_iota(jnp.int32, (rows, keys), 0)
            col = lax.broadcasted_iota(jnp.int32, (rows, keys), 1)
            slot = col // rows
            other = lax.rem(c - slot + m, m)
            limit = jnp.where(slot == 0, row, jnp.where((other < c) if half == LOW else (other > c), keys, -1))
            bias = jnp.where(col <= limit, 0.0, -jnp.inf)
            s = (score(0).reshape(heads, rows, keys) + bias[None]).reshape(heads * rows, keys)
            scores[0] = s
            row_max[...] = functools.reduce(jnp.maximum, [s[:, a : a + 128] for a in lanes])

            @pl.loop(1, count + 1)
            def _(i):
                s = score(i)
                scores[i] = s
                row_max[...] = functools.reduce(jnp.maximum, [s[:, a : a + 128] for a in lanes], row_max[...])

            top = jnp.max(row_max[...], axis=-1, keepdims=True) * to_log2
            row_max[...] = jnp.broadcast_to(top, row_max.shape)
            row_sum[...] = jnp.zeros_like(row_sum)
            acc_ref[...] = jnp.zeros_like(acc_ref)

            @pl.loop(0, count + 1)
            def _(i):
                top = row_max[...]
                e = [jnp.exp2(scores[i, :, a : a + 128] * to_log2 - top) for a in lanes]
                row_sum[...] += functools.reduce(jnp.add, e)
                weights = jnp.concatenate([x.astype(BF16) for x in e], axis=-1)
                acc_ref[...] += jnp.dot(weights, vs[group(i)], preferred_element_type=F32)

            out = (acc_ref[...] / jnp.sum(row_sum[...], axis=-1, keepdims=True)).astype(BF16)
            for h in range(heads):
                pieces[half, row_block(plane), h * hd : (h + 1) * hd] = out[h * rows : (h + 1) * rows]

    share = hc // m

    def wo_rows(plane, quarter):
        return pl.ds(pl.multiple_of(plane * hc + quarter * share, 16), share)

    def wo_copy(layer, s):
        src = w_o.at[layer, pl.ds(pl.multiple_of(c * share, 16), share), col_block(ring(z + s, n), width)]
        return remote(src, wo_cols.at[layer, wo_rows(z, c)], osend.at[layer, s - 1], orecv.at[layer, s - 1], tp=ring(z + s, n))

    def wo_pass(layer, s, j):
        here = wo_cols.at[layer, wo_rows(ring(z - s, n), c)]
        return remote(here, here, psend.at[layer, s - 1, j - 1], precv.at[layer, s - 1, j - 1], cp=ring(c + j, m))

    def wo_start(layer):
        for s in range(1, n):
            wo_copy(layer, s).start()

    def wo_event(layer):
        for s in range(1, n):
            wo_copy(layer, s).wait_recv()
            for j in range(1, m):
                wo_pass(layer, s, j).start()

    def wo_wait(layer):
        for s in range(1, n):
            for j in range(1, m):
                wo_pass(layer, s, j).wait_recv()

    span = d // PARTS

    def sum_slot(way, k):
        return k - 1 if way == UP else (0, 3, 4)[k - 1]

    def sum_copy(layer, half, way, q, k, block):
        cols = pl.ds(q * span, span)
        return remote(part.at[half, row_block(block), cols], sums.at[half, sum_slot(way, k), :, cols],
                      rsend.at[layer, half, way, q, k - 1], rrecv.at[layer, half, way, q, k - 1], tp=above if way == UP else below)

    def sum_start(layer, half, q):
        @pl.when(z == 0)
        def _():
            for k in range(1, n):
                sum_copy(layer, half, UP, q, k, n - k).start()

        @pl.when(z == n - 1)
        def _():
            for k in range(1, n):
                sum_copy(layer, half, DOWN, q, k, k - 1).start()

    def sum_event(layer, half, q, k):
        for way, here, block, more in ((UP, both(z >= 1, k >= z), n - 1 + z - k, z < n - 1),
                                       (DOWN, both(z <= n - 2, k >= n - 1 - z), z + k - n + 1, z > 0)):
            block = jnp.clip(block, 0, n - 1)

            @pl.when(here)
            def _(way=way, block=block):
                sum_copy(layer, half, way, q, k, block).wait_recv()
                step = 16

                @pl.loop(0, rows // step)
                def _(i):
                    to = pl.ds(pl.multiple_of(block * rows + i * step, step), step)
                    frm = pl.ds(pl.multiple_of(i * step, step), step)
                    part[half, to, q * span : (q + 1) * span] += sums[half, sum_slot(way, k), frm, q * span : (q + 1) * span]

            if k < n - 1:
                @pl.when(both(here, more))
                def _(way=way, block=block):
                    sum_copy(layer, half, way, q, k + 1, block).start()

    def sum_drain(layer, half):
        for q in range(PARTS):
            for k in range(1, n):
                @pl.when(both(z < n - 1, jnp.logical_or(z == 0, k - 1 >= z)))
                def _(q=q, k=k):
                    sum_copy(layer, half, UP, q, k, 0).wait_send()

                @pl.when(both(z > 0, jnp.logical_or(z == n - 1, k - 1 >= n - 1 - z)))
                def _(q=q, k=k):
                    sum_copy(layer, half, DOWN, q, k, 0).wait_send()

    def finish(half):
        step = 16

        @pl.loop(0, rows // step)
        def _(i):
            r = pl.ds(pl.multiple_of(i * step, step), step)
            mine = part[half, pl.ds(pl.multiple_of(z * rows + i * step, step), step)]
            home[half, r] = (home[half, r].astype(F32) + mine).astype(BF16)

    barrier = pltpu.get_barrier_semaphore()
    for s in (1, n - 1):
        pl.semaphore_signal(barrier, inc=1, device_id={"tp": ring(z + s, n)}, device_id_type=MESH)
    if n > 3:
        pl.semaphore_signal(barrier, inc=1, device_id={"tp": ring(z + 2, n)}, device_id_type=MESH)
    for s in range(1, m):
        pl.semaphore_signal(barrier, inc=1, device_id={"cp": ring(c + s, m)}, device_id_type=MESH)
    pl.semaphore_wait(barrier, n - 1 + m - 1)

    items = []

    def do(f, *args):
        items.append(("do", functools.partial(f, *args), None))

    def op(o, *hooks):
        items.append(("op", o, hooks))
        return o

    def pre(o):
        items.append(("pre", o, None))

    def ev(gather, k):
        return functools.partial(gather.event, k)

    def sums_ev(layer, half, k):
        def f():
            for q in range(PARTS):
                sum_event(layer, half, q, k)
        return f

    A, B = LOW, HIGH
    gate_tiles = ff // 128
    down_tiles = d // TILE

    def part_of(tiles, share):
        return min(tiles - 1, int(tiles * share))

    l = 0
    do(gx[l, A].start)
    qa = Qkv(l, A)
    pre(qa)
    do(gx[l, A].event, 1)
    do(gx[l, A].event, 2)
    do(wo_start, l)
    do(gx[l, B].start)
    do(gx[l, A].event, 3)
    do(norm_x, l, A)
    op(qa, (2, functools.partial(kv_start, l, A)))
    do(gx[l, B].event, 1)
    do(attend, l, A)
    do(go[l, A].start)
    do(wo_event, l)
    do(gx[l, B].event, 2)
    do(gx[l, B].event, 3)
    do(norm_x, l, B)
    op(Qkv(l, B), (2, functools.partial(kv_start, l, B)))
    do(go[l, A].event, 1)
    do(attend, l, B)
    do(go[l, A].event, 2)
    do(wo_wait, l)
    wa = Wo(l, A)
    pre(wa)
    do(go[l, A].event, 3)

    def o_to_h(l, half, o):
        do(load_cols, go[l, half], hc)
        do(go[l, half].drain, (0,))
        op(o)
        do(gh[l, half].start)

    def back_a(l):
        do(gh[l, A].event, 1)
        do(gh[l, A].event, 2)
        do(go[l, B].start)
        do(gh[l, A].event, 3)
        do(norm_h, l, A)
        op(GateUp(l, A), (part_of(gate_tiles, 0.35), ev(go[l, B], 1)), (part_of(gate_tiles, 0.9), ev(go[l, B], 2)))
        if l > 0:
            do(sum_drain, l - 1, A)
        op(Down(l, A), (down_tiles // 2, functools.partial(sum_start, l, A, 0)), (part_of(down_tiles, 0.75), ev(go[l, B], 3)))
        do(sum_start, l, A, 1)
        o_to_h(l, B, Wo(l, B))
        do(gh[l, B].event, 1)
        do(sums_ev(l, A, 1))
        do(gh[l, B].event, 2)
        do(gh[l, B].event, 3)
        do(norm_h, l, B)

    o_to_h(l, A, wa)
    back_a(l)
    do(wo_start, 1)
    op(GateUp(l, B), (part_of(gate_tiles, 0.3), sums_ev(l, A, 2)), (part_of(gate_tiles, 0.6), functools.partial(wo_event, 1)))
    op(Down(l, B), (part_of(down_tiles, 0.3), sums_ev(l, A, 3)), (down_tiles // 2, functools.partial(sum_start, l, B, 0)))
    do(sum_start, l, B, 1)
    do(finish, A)
    do(gx[1, A].start)

    l = 1
    do(gx[l, A].event, 1)
    do(gx[l, A].event, 2)
    do(wo_wait, l)
    do(gx[l, A].event, 3)
    do(norm_x, l, A)
    op(Qkv(l, A), (2, functools.partial(kv_start, l, A)))
    do(sums_ev(0, B, 1))
    do(attend, l, A)
    do(go[l, A].start)
    do(sums_ev(0, B, 2))
    do(go[l, A].event, 1)
    do(sums_ev(0, B, 3))
    do(finish, B)
    do(go[l, A].event, 2)
    do(gx[l, B].start)
    do(go[l, A].event, 3)
    o_to_h(l, A, Wo(l, A))
    do(gx[l, B].event, 1)
    do(gh[l, A].event, 1)
    do(gx[l, B].event, 2)
    do(gx[l, B].event, 3)
    do(norm_x, l, B)
    op(Qkv(l, B), (2, functools.partial(kv_start, l, B)))
    do(gh[l, A].event, 2)
    do(attend, l, B)
    do(go[l, B].start)
    do(gh[l, A].event, 3)
    do(norm_h, l, A)
    op(GateUp(l, A), (part_of(gate_tiles, 0.1), ev(go[l, B], 1)), (part_of(gate_tiles, 0.5), ev(go[l, B], 2)),
       (part_of(gate_tiles, 0.9), ev(go[l, B], 3)))
    do(sum_drain, 0, A)
    op(Down(l, A), (down_tiles // 2, functools.partial(sum_start, l, A, 0)))
    do(sum_start, l, A, 1)
    o_to_h(l, B, Wo(l, B))
    do(gh[l, B].event, 1)
    do(sums_ev(l, A, 1))
    do(gh[l, B].event, 2)
    do(gh[l, B].event, 3)
    do(norm_h, l, B)
    op(GateUp(l, B), (part_of(gate_tiles, 0.4), sums_ev(l, A, 2)))
    do(sum_drain, 0, B)
    op(Down(l, B), (part_of(down_tiles, 0.3), sums_ev(l, A, 3)), (down_tiles // 2, functools.partial(sum_start, l, B, 0)))
    do(sum_start, l, B, 1)
    do(finish, A)

    def put(half, wait):
        copy = pltpu.make_async_copy(home.at[half], y_out.at[pl.ds(half * rows, rows)], lsem.at[half])
        copy.wait() if wait else copy.start()

    do(put, A, False)
    for k in range(1, n):
        do(sums_ev(l, B, k))
    do(finish, B)
    do(put, B, False)
    do(sum_drain, l, A)
    do(sum_drain, l, B)
    for i in range(layers):
        for half in (A, B):
            do(gx[i, half].drain, (0, 1, 2) if i == 0 else (1, 2))
            do(go[i, half].drain, (1, 2))
            do(gh[i, half].drain, (1, 2))

    def last_sends():
        for i in range(layers):
            for half in (A, B):
                for s in range(1, m):
                    kv_copy(i, half, s).wait_send()
            for s in range(1, n):
                wo_copy(i, s).wait_send()
                for j in range(1, m):
                    wo_pass(i, s, j).wait_send()

    do(last_sends)
    do(put, A, True)
    do(put, B, True)

    ops = [o for what, o, _ in items if what == "op"]
    named = [o for what, o, _ in items if what == "pre"]
    base = 0
    for o in ops:
        o.base = base % SLOTS
        base += o.tiles
    follow = {id(o): (f if f not in named else None) for o, f in zip(ops, ops[1:])}
    for what, o, hooks in items:
        if what == "do":
            o()
        elif what == "pre":
            o.prefetch()
        else:
            o.run(follow.get(id(o)), hooks)


def solution(mesh):
    n = mesh.shape['tp']
    m = mesh.shape['cp']
    row_spec = P(('dp', 'tp', 'cp'), None)
    gain_spec = P(None, None)
    q_spec = P(None, None, 'tp', None)
    col_spec = P(None, None, 'tp')
    o_spec = P(None, 'tp', None, None)
    down_spec = P(None, 'tp', None)

    def body(tokens, norm_attn, norm_mlp, w_q, w_k, w_v, w_o, w_gate, w_up, w_down):
        layers, d, heads, hd = w_q.shape
        rows = tokens.shape[0] // 2
        hc = heads * hd
        width = d // n
        ff = w_gate.shape[2]
        all_rows = n * rows
        c = lax.axis_index('cp')

        inv_freq = 500000.0 ** (-(jnp.arange(hd // 2, dtype=F32) * 2.0 / hd))
        seg = jnp.arange(n) * m + c
        seg = jnp.stack([seg, 2 * n * m - 1 - seg])
        pos = (seg[:, :, None] * rows + jnp.arange(rows)).reshape(2, all_rows)
        angle = pos.astype(F32)[..., None] * inv_freq
        cos, sin = jnp.cos(angle), jnp.sin(angle)
        cos, sin = jnp.concatenate([cos, cos], -1), jnp.concatenate([-sin, sin], -1)

        hbm = pl.BlockSpec(memory_space=pl.ANY)
        vmem = pl.BlockSpec(memory_space=pltpu.VMEM)
        dma = pltpu.SemaphoreType.DMA
        out = pl.pallas_call(
            functools.partial(kernel, n, m, layers),
            out_shape=(
                jax.ShapeDtypeStruct(tokens.shape, BF16),
                jax.ShapeDtypeStruct((layers, 2, n, rows, d), BF16),
                jax.ShapeDtypeStruct((layers, 2, n, all_rows, hc), BF16),
                jax.ShapeDtypeStruct((layers, 2, n, all_rows, width), BF16),
                jax.ShapeDtypeStruct((layers, n * hc, width), BF16),
            ),
            in_specs=[hbm, vmem, vmem, vmem, vmem] + [hbm] * 7,
            out_specs=(hbm,) * 5,
            scratch_shapes=[
                pltpu.VMEM((all_rows, d), BF16),
                pltpu.VMEM((all_rows, d), BF16),
                pltpu.VMEM((all_rows, ff), BF16),
                pltpu.VMEM((2, all_rows, d), F32),
                pltpu.VMEM((2, 5, rows, d), F32),
                pltpu.VMEM((2 * n, heads * rows, m * rows), F32),
                pltpu.VMEM((2 * n, m * rows, hd), BF16),
                pltpu.VMEM((2 * n, m * rows, hd), BF16),
                pltpu.VMEM((layers, 2, m, all_rows, 2 * hd), BF16),
                pltpu.VMEM((n, heads * rows, hd), BF16),
                pltpu.VMEM((2, all_rows, width), BF16),
                pltpu.VMEM((2, all_rows, width), BF16),
                pltpu.VMEM((2, rows, d), BF16),
                pltpu.VMEM((SLOTS, max(d, ff), TILE), BF16),
                pltpu.VMEM((heads * rows, 128), F32),
                pltpu.VMEM((heads * rows, 128), F32),
                pltpu.VMEM((heads * rows, hd), F32),
                dma((SLOTS, n)),
                dma((n,)),
                dma((layers * 6, 2, n - 1)),
                dma((layers * 6, 2, n - 1)),
                dma((layers, 2, m - 1)),
                dma((layers, 2, m - 1)),
                dma((layers, 2, 2, PARTS, n - 1)),
                dma((layers, 2, 2, PARTS, n - 1)),
                dma((layers, n - 1)),
                dma((layers, n - 1)),
                dma((layers, n - 1, m - 1)),
                dma((layers, n - 1, m - 1)),
            ],
            compiler_params=pltpu.CompilerParams(collective_id=0, has_side_effects=True, vmem_limit_bytes=67043328),
            name="two_layers",
        )(tokens, norm_attn, norm_mlp, cos, sin, w_q.reshape(layers, d, hc), w_k, w_v, w_o.reshape(layers, hc, d), w_gate, w_up, w_down)
        return out[0]

    return jax.shard_map(
        body,
        mesh=mesh,
        in_specs=(row_spec, gain_spec, gain_spec, q_spec, col_spec, col_spec, o_spec, col_spec, col_spec, down_spec),
        out_specs=row_spec,
        check_vma=False,
    )
```

time: 1670 us -> 1220 us (0.73)
  Pallas kernels: 0 us -> 1170 us
  waiting for transfers between devices: 1120 us -> 0 us
  matrix products: 346 us -> 0 us
  other arithmetic: 79.8 us -> 3.35 us
  blocking collectives: 35 us -> 0 us
  local copies, waits for them, and re-layouts: 66.3 us -> 38.8 us
    pallas_call x0 -> x1, Pallas kernels: none -> 1170 us  [body(): pl.pallas_call(functools.partial(kernel, n, m, layers), out_shape=(jax.Sh...]
    reduce_scatter x4 -> x0, waiting for transfers between devices: 738 us -> none  [the longest x2 370 us: body(): mlp_out = lax.psum_scatter(mlp_part, 'tp', scatter_dimension=0, tiled=True)]
    all_gather x4 -> x0, waiting for transfers between devices: 380 us -> none  [the longest x2 205 us: body(): lax.all_gather(rms_norm(hidden_mid, norm_mlp[layer_idx]), 'tp', axis=0, t...]
    dot_general x44 -> x0, matrix products: 328 us -> none  [the longest x2 74.8 us: body(): jnp.dot(normed_mlp, w_up[layer_idx], preferred_element_type=jnp.float32)]
    reduce_sum x20 -> x0, other arithmetic: 42.9 us -> none  [the longest x16 34.4 us: one_block(): row_sum = jnp.sum(weights, axis=-1, keepdims=True)]
    all_gather x4 -> x0, blocking collectives: 35 us -> none  [the longest x2 17.8 us: body(): values_all = lax.all_gather(values_loc, 'cp', axis=0, tiled=True)]
    reshape x0 -> x1, local copies, waits for them, and re-layouts: none -> 18 us  [body(): w_q.reshape(layers, d, hc)]
    unnamed x2 -> x0, matrix products: 17.9 us -> none
  transfers between devices with their start and end apart: 8 -> 0, of which waited for: 8 -> 0; matrix products, arithmetic and copies ran while one was open for 2% -> 0% of each run, Pallas kernels for 0% -> 0%
where the time goes in v1:
time: 1220 us; the launch traced here: 1210 us
  Pallas kernels  1170 us (96%)
  local copies, waits for them, and re-layouts  38.8 us (3%)
    pallas_call x1, Pallas kernels, body(): pl.pallas_call(functools.partial(kernel, n, m, layers), out_shape=(jax.Sh...  1170 us

profile of v1, /device:TPU:0, one launch (start us, length us, event | category | flops | bytes accessed | tf_op | source)
XLA Modules:
  0.0 1211.1 jit_solution(6409126967820100457)
XLA Ops:
  0.0 0.1 add.50
  0.1 0.1 add.47
  0.2 0.1 add.48
  0.3 1.5 fusion
  1.7 0.9 pad_maximum_fusion.1.sin_ref
  2.7 0.9 pad_maximum_fusion.cos_ref
  3.6 18.0 %copy.12 = bf16[2,3584,7,128]{1,3,2,0:T(8,128)(2,1)} copy(bf16[2,3584,7,128]{3,1,2,0:T(8,128)(2,1)} %param.13) | data formatting | bytes 25690112 | tf_op args[3]
  21.6 18.0 %copy.13.w_q = bf16[2,3584,896]{2,1,0:T(8,128)(2,1)} copy(bf16[2,3584,896]{1,2,0:T(8,128)(2,1)} %bitcast.2) | data formatting | bytes 25690112 | tf_op jit(solution)/shard_map/reshape | solution.py:704
  39.7 1168.9 %two_layers.1 = (bf16[192,3584]{1,0:T(8,128)(2,1)}, bf16[2,2,4,96,3584]{4,3,2,1,0:T(8,128)(2,1)}, bf16[2,2,4,384,896]{4,3,2,1,0:T(8,128)(2,1)}, bf16[2,2,4,384,8...) custom-call(bf16[192,3584]{1,0:T(8,128)(2,1)} %tokens.1, bf16[2,3584]{1,0:T(2,128)(2,1)} %gain_a.1, bf16[2,3584]{1,0:T(2,128)(2,1)} %gain_m.1, ...), custom_call_target="tpu_custom_call" | custom-call | tf_op jit(solution)/shard_map/two_layers/pallas_call | solution.py:660
  1208.6 2.5 copy.15
  (5 shorter events, 0.0 us)
